TPU v7x, 256 devices: a whole 4x4x8 slice. The times are simulated.
256 devices in a mesh: dp: 16 (over x_hi, z), param: 16 (over y, x_lo, core).
Axes of the slice: x: 4 (x_hi: 2, x_lo: 2; x = x_hi * 2 + x_lo), y: 4, z: 8, core: 2. Of those that a mesh axis runs over, the one named last changes fastest.
Arguments:
- ex_grads: bfloat16 [1536, 20480], P('dp', 'param'), may hold values from -6 to 6
- tgt_grads: bfloat16 [4096, 20480], P('dp', 'param'), may hold values from -6 to 6
- projection: bfloat16 [20480, 4096], P('param'), may hold values from -0.0390625 to 0.0390625
- example_weight: float32 [1536], P('param'), may hold values from 0.05 to 1
Outputs:
- scores: float32 [4096, 1536], P('dp', 'param')
All inputs are finite; a program needn't handle non-finite values.
Results may differ from a plain program's by a relative error of at most 0.0078.
Values may be sent and summed in bfloat16 or wider, within the bound.
A program may use at most 192 MiB of HBM per device.

v0:
```python
import math
import jax
import jax.numpy as jnp
from jax import lax
from jax.sharding import PartitionSpec as P

ridge_value = 0.5


def sent_to_all(x, axis):
    length = lax.axis_size(axis)
    return lax.all_to_all(jnp.broadcast_to(x[None], (length, *x.shape)), axis, 0, 0, tiled=True)


def in_order(parts, dim):
    parts = jnp.moveaxis(parts, 0, dim)
    lengths = parts.shape
    return parts.reshape(*lengths[:dim], lengths[dim] * lengths[dim + 1], *lengths[dim + 2 :])


def gather_directly(x, axis, dim):
    parts = sent_to_all(x, axis)
    return in_order(parts, dim)


def with_ridge(block, first_row):
    row_ids = lax.broadcasted_iota(jnp.int32, block.shape, 0) + first_row
    col_ids = lax.broadcasted_iota(jnp.int32, block.shape, 1)
    return block + jnp.where(row_ids == col_ids, ridge_value, 0.0).astype(jnp.float32)


def on_device(ex_grads, tgt_grads, projection, example_weight):
    ex_rows = ex_grads.shape[0]
    columns = projection.shape[1]
    param_total = lax.axis_size("param")
    param_pos = lax.axis_index("param")
    replica_pos = lax.axis_index("dp")
    stacked = jnp.concatenate([ex_grads, tgt_grads], axis=0)
    contract_rows = (((0,), (1,)), ((), ()))
    feature_block = lax.psum_scatter(
        lax.dot_general(projection, stacked, contract_rows, preferred_element_type=jnp.float32),
        "param",
        scatter_dimension=0,
        tiled=True,
    )
    local_features = feature_block.astype(jnp.bfloat16)
    example_part = local_features[:, :ex_rows]
    contract_first = (((0,), (0,)), ((), ()))
    partial_value = lax.dot_general(
        local_features,
        gather_directly(example_part, "dp", 1),
        contract_first,
        preferred_element_type=jnp.float32,
    )
    examples = partial_value.shape[1]
    summed = lax.psum(partial_value, "param")
    kernel_block = with_ridge(summed[:ex_rows] / columns, replica_pos * ex_rows)
    kernel = lax.all_gather(kernel_block, "dp", axis=0, tiled=True)
    cross_terms = summed[ex_rows:] / columns
    factor = jnp.linalg.cholesky(kernel)
    forward = jax.scipy.linalg.solve_triangular(factor, cross_terms.T, lower=True)
    solved = jax.scipy.linalg.solve_triangular(factor, forward, lower=True, trans=1)
    block_cols = examples // param_total
    chosen = lax.dynamic_slice_in_dim(solved.T, param_pos * block_cols, block_cols, 1)
    return chosen * math.sqrt(columns) * example_weight[None, :]


def solution(mesh):
    placed = (P("dp", "param"), P("dp", "param"), P("param", None), P("param"))
    return jax.shard_map(
        on_device, mesh=mesh, in_specs=placed, out_specs=P("dp", "param"), check_vma=False
    )
```

profile of v0, /device:TPU:1, one launch (start us, length us, event | category | flops | bytes accessed | tf_op | source)
XLA Modules:
  0.0 965.1 jit_solution(2935307158991540555)
XLA Ops:
  6.5 10.7 %convolution_bitcast_fusion = f32[4096,352]{0,1:T(8,128)} fusion(bf16[1280,4096]{1,0:T(8,128)(2,1)} %param.6, bf16[256,1280]{1,0:T(8,128)(2,1)} %param.5, bf16[96,1280]{1,0:T(8,128)(2,1)} %param.4), kind=kOutput, calls=%fused_computation.6 | convolution fusion | flops 3692789760 | bytes 17154048 | tf_op jit(solution)/shard_map/dot_general | solution.py:41
  17.3 79.7 %reduce-scatter.2.cloned.1.call-done = f32[256,352]{0,1:T(8,128)} async-done(((f32[4096,352]{0,1:T(8,128)}), f32[256,352]{0,1:T(8,128)}) %reduce-scatter.2.cloned.1.call-update) | async-done | bytes 360464 | tf_op jit(solution)/shard_map/reduce_scatter | solution.py:40
  98.1 27.1 %all_to_all.5 = bf16[16,256,96]{1,2,0:T(8,128)(2,1)S(1)} all-to-all(bf16[16,256,96]{1,2,0:T(8,128)(2,1)S(1)} %broadcast_in_dim.17), channel_id=1, replica_groups=mesh['dp'=16,'param'=16] {'dp'}, dimensions={0} | all-to-all | bytes 1572864 | tf_op jit(solution)/shard_map/all_to_all | solution.py:12
  127.1 130.4 %all-reduce.3.cloned.1.call-done = f32[352,1536]{1,0:T(8,128)} async-done(((f32[352,1536]{1,0:T(8,128)}), f32[352,1536]{1,0:T(8,128)}) %all-reduce.3.cloned.1.call-update) | async-done | bytes 2162704 | tf_op jit(solution)/shard_map/psum | solution.py:56
  261.1 144.9 %all-gather.2.cloned.1.call-done = f32[1536,1536]{1,0:T(8,128)} async-done(((f32[96,1536]{1,0:T(8,128)}), f32[1536,1536]{1,0:T(8,128)}) %all-gather.2.cloned.1.call-update) | async-done | bytes 9437200 | tf_op jit(solution)/shard_map/all_gather | solution.py:58
  406.0 10.1 %copy.10 = f32[1536,1536]{0,1:T(8,128)} copy(f32[1536,1536]{1,0:T(8,128)} %all-gather.2.cloned.1.call-done) | data formatting | bytes 18874368 | tf_op jit(solution)/shard_map/all_gather | solution.py:58
  416.1 12.3 %fusion = f32[1536,1536]{1,0:T(8,128)} fusion(f32[1536,1536]{1,0:T(8,128)} %all-gather.2.cloned.1.call-done, f32[1536,1536]{0,1:T(8,128)} %copy.10), kind=kLoop, calls=%fused_computation.4 | loop fusion | flops 4718592 | bytes 28311552 | tf_op jit(solution)/shard_map/jit(cholesky)/div | solution.py:60
  429.3 11.7 %cholesky.341 = f32[128,128]{1,0:T(8,128)S(1)} custom-call(f32[128,128]{1,0:T(8,128)S(1)} %cholesky.892), custom_call_target="Cholesky" | custom-call | tf_op jit(solution)/shard_map/jit(cholesky)/cholesky | solution.py:60
  445.8 9.8 %custom-call.98 = f32[1,128,128]{1,2,0:T(8,128)S(1)} custom-call(f32[1,128,128]{2,1,0:T(8,128)S(1)} %get-tuple-element.111), custom_call_target="InvertDiagBlocksLowerTriangular" | custom-call | tf_op jit(solution)/shard_map/jit(cholesky)/cholesky | solution.py:60
  460.3 11.9 %cholesky.362 = f32[128,128]{1,0:T(8,128)S(1)} custom-call(f32[128,128]{1,0:T(8,128)S(1)} %cholesky.896), custom_call_target="Cholesky" | custom-call | tf_op jit(solution)/shard_map/jit(cholesky)/cholesky | solution.py:60
  472.9 9.8 %custom-call.99 = f32[1,128,128]{1,2,0:T(8,128)S(1)} custom-call(f32[1,128,128]{2,1,0:T(8,128)S(1)} %get-tuple-element.108), custom_call_target="InvertDiagBlocksLowerTriangular" | custom-call | tf_op jit(solution)/shard_map/jit(cholesky)/cholesky | solution.py:60
  487.0 11.7 %cholesky.385 = f32[128,128]{1,0:T(8,128)S(1)} custom-call(f32[128,128]{1,0:T(8,128)S(1)} %cholesky.901), custom_call_target="Cholesky" | custom-call | tf_op jit(solution)/shard_map/jit(cholesky)/cholesky | solution.py:60
  499.4 10.0 %custom-call.100 = f32[1,128,128]{1,2,0:T(8,128)S(1)} custom-call(f32[1,128,128]{2,1,0:T(8,128)S(1)} %get-tuple-element.105), custom_call_target="InvertDiagBlocksLowerTriangular" | custom-call | tf_op jit(solution)/shard_map/jit(cholesky)/cholesky | solution.py:60
  514.3 11.7 %cholesky.715 = f32[128,128]{1,0:T(8,128)S(1)} custom-call(f32[128,128]{1,0:T(8,128)S(1)} %cholesky.906), custom_call_target="Cholesky" | custom-call | tf_op jit(solution)/shard_map/jit(cholesky)/cholesky | solution.py:60
  526.6 9.8 %custom-call.101 = f32[1,128,128]{1,2,0:T(8,128)S(1)} custom-call(f32[1,128,128]{2,1,0:T(8,128)S(1)} %get-tuple-element.102), custom_call_target="InvertDiagBlocksLowerTriangular" | custom-call | tf_op jit(solution)/shard_map/jit(cholesky)/cholesky | solution.py:60
  541.4 12.1 %cholesky.734 = f32[128,128]{1,0:T(8,128)S(1)} custom-call(f32[128,128]{1,0:T(8,128)S(1)} %cholesky.911), custom_call_target="Cholesky" | custom-call | tf_op jit(solution)/shard_map/jit(cholesky)/cholesky | solution.py:60
  554.2 9.8 %custom-call.102 = f32[1,128,128]{1,2,0:T(8,128)S(1)} custom-call(f32[1,128,128]{2,1,0:T(8,128)S(1)} %get-tuple-element.99), custom_call_target="InvertDiagBlocksLowerTriangular" | custom-call | tf_op jit(solution)/shard_map/jit(cholesky)/cholesky | solution.py:60
  569.1 11.7 %cholesky.754 = f32[128,128]{1,0:T(8,128)S(1)} custom-call(f32[128,128]{1,0:T(8,128)S(1)} %cholesky.916), custom_call_target="Cholesky" | custom-call | tf_op jit(solution)/shard_map/jit(cholesky)/cholesky | solution.py:60
  581.5 10.0 %custom-call.103 = f32[1,128,128]{1,2,0:T(8,128)S(1)} custom-call(f32[1,128,128]{2,1,0:T(8,128)S(1)} %get-tuple-element.96), custom_call_target="InvertDiagBlocksLowerTriangular" | custom-call | tf_op jit(solution)/shard_map/jit(cholesky)/cholesky | solution.py:60
  596.6 11.7 %cholesky.774 = f32[128,128]{1,0:T(8,128)S(1)} custom-call(f32[128,128]{1,0:T(8,128)S(1)} %cholesky.921), custom_call_target="Cholesky" | custom-call | tf_op jit(solution)/shard_map/jit(cholesky)/cholesky | solution.py:60
  609.0 9.8 %custom-call.104 = f32[1,128,128]{1,2,0:T(8,128)S(1)} custom-call(f32[1,128,128]{2,1,0:T(8,128)S(1)} %get-tuple-element.93), custom_call_target="InvertDiagBlocksLowerTriangular" | custom-call | tf_op jit(solution)/shard_map/jit(cholesky)/cholesky | solution.py:60
  624.1 11.7 %cholesky.794 = f32[128,128]{1,0:T(8,128)S(1)} custom-call(f32[128,128]{1,0:T(8,128)S(1)} %cholesky.926), custom_call_target="Cholesky" | custom-call | tf_op jit(solution)/shard_map/jit(cholesky)/cholesky | solution.py:60
  636.5 9.8 %custom-call.105 = f32[1,128,128]{1,2,0:T(8,128)S(1)} custom-call(f32[1,128,128]{2,1,0:T(8,128)S(1)} %get-tuple-element.90), custom_call_target="InvertDiagBlocksLowerTriangular" | custom-call | tf_op jit(solution)/shard_map/jit(cholesky)/cholesky | solution.py:60
  650.9 12.2 %cholesky.814 = f32[128,128]{1,0:T(8,128)S(1)} custom-call(f32[128,128]{1,0:T(8,128)S(1)} %cholesky.931), custom_call_target="Cholesky" | custom-call | tf_op jit(solution)/shard_map/jit(cholesky)/cholesky | solution.py:60
  663.7 9.8 %custom-call.106 = f32[1,128,128]{1,2,0:T(8,128)S(1)} custom-call(f32[1,128,128]{2,1,0:T(8,128)S(1)} %get-tuple-element.87), custom_call_target="InvertDiagBlocksLowerTriangular" | custom-call | tf_op jit(solution)/shard_map/jit(cholesky)/cholesky | solution.py:60
  677.9 11.7 %cholesky.834 = f32[128,128]{1,0:T(8,128)S(1)} custom-call(f32[128,128]{1,0:T(8,128)S(1)} %cholesky.936), custom_call_target="Cholesky" | custom-call | tf_op jit(solution)/shard_map/jit(cholesky)/cholesky | solution.py:60
  690.2 9.8 %custom-call.107 = f32[1,128,128]{1,2,0:T(8,128)S(1)} custom-call(f32[1,128,128]{2,1,0:T(8,128)S(1)} %get-tuple-element.84), custom_call_target="InvertDiagBlocksLowerTriangular" | custom-call | tf_op jit(solution)/shard_map/jit(cholesky)/cholesky | solution.py:60
  703.7 11.9 %cholesky.854 = f32[128,128]{1,0:T(8,128)S(1)} custom-call(f32[128,128]{1,0:T(8,128)S(1)} %cholesky.941), custom_call_target="Cholesky" | custom-call | tf_op jit(solution)/shard_map/jit(cholesky)/cholesky | solution.py:60
  716.2 9.8 %custom-call.108 = f32[1,128,128]{1,2,0:T(8,128)S(1)} custom-call(f32[1,128,128]{2,1,0:T(8,128)S(1)} %get-tuple-element.81), custom_call_target="InvertDiagBlocksLowerTriangular" | custom-call | tf_op jit(solution)/shard_map/jit(cholesky)/cholesky | solution.py:60
  729.2 11.7 %cholesky.872 = f32[128,128]{1,0:T(8,128)S(1)} custom-call(f32[128,128]{1,0:T(8,128)S(1)} %convolution_subtract_fusion.25), custom_call_target="Cholesky" | custom-call | tf_op jit(solution)/shard_map/jit(cholesky)/cholesky | solution.py:60
  765.2 35.2 %while.1 = (s32[]{:T(128)}, f32[1536,1536]{1,0:T(8,128)}, s32[12,2]{0,1:T(2,128)S(1)}, f32[12,128,128]{2,1,0:T(8,128)S(1)}, s32[]{:T(128)}) while((s32[]{:T(128)}, f32[1536,1536]{1,0:T(8,128)}, s32[12,2]{0,1:T(2,128)S(1)}, f32[12,128,128]{2,1,0:T(8,128)S(1)}, s32[]{:T(128)}) %tuple.106), condition=%wide.while_cond, body=%wide.while_body.sunk | while | flops 2 | bytes 131189 | solution.py:62
  800.4 118.3 %custom-call.109 = f32[12,128,128]{1,2,0:T(8,128)S(1)} custom-call(f32[12,128,128]{2,1,0:T(8,128)S(1)} %get-tuple-element.12), custom_call_target="InvertDiagBlocksLowerTriangular" | custom-call | tf_op jit(solution)/shard_map/jit(_solve_triangular)/triangular_solve | solution.py:62
  (222 shorter events, 159.5 us)
Async XLA Ops:
  6.5 90.4 %reduce-scatter.2.cloned.1.call-start = ((), (), s32[]{:S(2)}) async-start(), calls=%async_computation.2 | async-start | bytes 6127616 | tf_op jit(solution)/shard_map/reduce_scatter | solution.py:40
  17.2 240.3 %all-reduce.3.cloned.1.call-start = ((), (), s32[]{:S(2)}) async-start(), calls=%async_computation.3 | async-start | bytes 4325376 | tf_op jit(solution)/shard_map/psum | solution.py:56
  127.0 132.5 %copy-start.1 = (f32[96]{0:T(128)S(1)}, f32[96]{0:T(128)}, u32[]{:S(2)}) copy-start(f32[96]{0:T(128)} %param.7) | copy-start | bytes 1156
  127.1 278.9 %all-gather.2.cloned.1.call-start = ((), (), s32[]{:S(2)}) async-start(), calls=%async_computation.4 | async-start | bytes 10027008 | tf_op jit(solution)/shard_map/all_gather | solution.py:58
  920.3 9.7 %copy-start = (f32[1536,1536]{1,0:T(8,128)S(1)}, f32[1536,1536]{1,0:T(8,128)}, u32[]{:S(2)}) copy-start(f32[1536,1536]{1,0:T(8,128)} %get-tuple-element.190) | copy-start | bytes 28311556
Sparse Core Ops, SparseCore 0:
  17.4 79.5 reduce-scatter.1
  127.2 130.2 all-reduce.2
  260.1 145.8 all-gather.1
where the time goes:
time: 970 us; the launch traced here: 965 us
  other arithmetic  409 us (42%)
  waiting for transfers between devices  355 us (37%)
  matrix products  100 us (10%)
  local copies, waits for them, and re-layouts  51.6 us (5%)
  blocking collectives  27.1 us (3%)
  between operations  22.1 us (2%)
    another operation x46, other arithmetic, on_device(): factor = jnp.linalg.cholesky(kernel)  265 us
    all_gather x1, waiting for transfers between devices, on_device(): kernel = lax.all_gather(kernel_block, 'dp', axis=0, tiled=True)  145 us
    psum x1, waiting for transfers between devices, on_device(): summed = lax.psum(partial_value, 'param')  130 us
    another operation x3, other arithmetic, on_device(): jax.scipy.linalg.solve_triangular(factor, forward, lower=True, trans=1)  127 us
    reduce_scatter x1, waiting for transfers between devices, on_device(): lax.psum_scatter(lax.dot_general(projection, stacked, contract_rows, pref...  79.7 us
    another operation x22, matrix products, on_device(): factor = jnp.linalg.cholesky(kernel)  50.1 us
    another operation x36, local copies, waits for them, and re-layouts  35 us
    all_to_all x1, blocking collectives, sent_to_all(): lax.all_to_all(jnp.broadcast_to(x[None], (length, *x.shape)), axis, 0, 0,...  27.1 us
  transfers between devices with their start and end apart: 3, of which 3 were waited for; matrix products, arithmetic and copies ran while one was open for 0% of the time, Pallas kernels for 0%

commit v1 on v0

--- a/solution.py
+++ b/solution.py
@@ -55,7 +55,9 @@
     examples = partial_value.shape[1]
     summed = lax.psum(partial_value, "param")
     kernel_block = with_ridge(summed[:ex_rows] / columns, replica_pos * ex_rows)
-    kernel = lax.all_gather(kernel_block, "dp", axis=0, tiled=True)
+    kernel = jnp.concatenate(
+        lax.all_to_all(jnp.stack([kernel_block] * lax.axis_size("dp")), "dp", 0, 0), axis=0
+    )
     cross_terms = summed[ex_rows:] / columns
     factor = jnp.linalg.cholesky(kernel)
     forward = jax.scipy.linalg.solve_triangular(factor, cross_terms.T, lower=True)

time: 970 us -> 1060 us (1.093); the launches traced: 965 us -> 1040 us
  waiting for transfers between devices: 355 us -> 417 us
    all_to_all x0 -> x1, waiting for transfers between devices: none -> 207 us  [on_device(): lax.all_to_all(jnp.stack([kernel_block] * lax.axis_size('dp')), 'dp', 0, 0)]
    all_gather x1 -> x0, waiting for transfers between devices: 145 us -> none  [on_device(): kernel = lax.all_gather(kernel_block, 'dp', axis=0, tiled=True)]
    another operation x36 -> x37, local copies, waits for them, and re-layouts: 35 us -> 39.7 us
where the time goes in v1:
time: 1060 us; the launch traced here: 1040 us
  waiting for transfers between devices  417 us (39%)
  other arithmetic  408 us (38%)
  matrix products  100 us (9%)
  local copies, waits for them, and re-layouts  56.4 us (5%)
  blocking collectives  27.1 us (3%)
  between operations  22.4 us (2%)
    another operation x46, other arithmetic, on_device(): factor = jnp.linalg.cholesky(kernel)  265 us
    all_to_all x1, waiting for transfers between devices, on_device(): lax.all_to_all(jnp.stack([kernel_block] * lax.axis_size('dp')), 'dp', 0, 0)  207 us
    psum x1, waiting for transfers between devices, on_device(): summed = lax.psum(partial_value, 'param')  130 us
    another operation x3, other arithmetic, on_device(): jax.scipy.linalg.solve_triangular(factor, forward, lower=True, trans=1)  127 us
    reduce_scatter x1, waiting for transfers between devices, on_device(): lax.psum_scatter(lax.dot_general(projection, stacked, contract_rows, pref...  79.7 us
    another operation x22, matrix products, on_device(): factor = jnp.linalg.cholesky(kernel)  50.1 us
    another operation x36, local copies, waits for them, and re-layouts  35 us
    all_to_all x1, blocking collectives, sent_to_all(): lax.all_to_all(jnp.broadcast_to(x[None], (length, *x.shape)), axis, 0, 0,...  27.1 us
  transfers between devices with their start and end apart: 3, of which 3 were waited for; matrix products, arithmetic and copies ran while one was open for 0% of the time, Pallas kernels for 0%

profile of v1, /device:TPU:1, one launch (start us, length us, event | category | flops | bytes accessed | tf_op | source)
XLA Modules:
  0.0 1040.4 jit_solution(2385448750648486340)
XLA Ops:
  6.5 10.7 %convolution_bitcast_fusion = f32[4096,352]{0,1:T(8,128)} fusion(bf16[1280,4096]{1,0:T(8,128)(2,1)} %param.6, bf16[256,1280]{1,0:T(8,128)(2,1)} %param.5, bf16[96,1280]{1,0:T(8,128)(2,1)} %param.4), kind=kOutput, calls=%fused_computation.6 | convolution fusion | flops 3692789760 | bytes 17154048 | tf_op jit(solution)/shard_map/dot_general | solution.py:41
  17.3 79.7 %reduce-scatter.2.cloned.1.call-done = f32[256,352]{0,1:T(8,128)} async-done(((f32[4096,352]{0,1:T(8,128)}), f32[256,352]{0,1:T(8,128)}) %reduce-scatter.2.cloned.1.call-update) | async-done | bytes 360464 | tf_op jit(solution)/shard_map/reduce_scatter | solution.py:40
  98.1 27.1 %all_to_all.10 = bf16[16,256,96]{1,2,0:T(8,128)(2,1)S(1)} all-to-all(bf16[16,256,96]{1,2,0:T(8,128)(2,1)S(1)} %broadcast_in_dim.17), channel_id=1, replica_groups=mesh['dp'=16,'param'=16] {'dp'}, dimensions={0} | all-to-all | bytes 1572864 | tf_op jit(solution)/shard_map/all_to_all | solution.py:12
  127.1 130.4 %all-reduce.3.cloned.1.call-done = f32[352,1536]{1,0:T(8,128)} async-done(((f32[352,1536]{1,0:T(8,128)}), f32[352,1536]{1,0:T(8,128)}) %all-reduce.3.cloned.1.call-update) | async-done | bytes 2162704 | tf_op jit(solution)/shard_map/psum | solution.py:56
  274.0 207.0 %all-to-all-done.1 = f32[16,96,1536]{2,1,0:T(8,128)} async-done(((f32[16,96,1536]{2,1,0:T(8,128)}), f32[16,96,1536]{2,1,0:T(8,128)}, u32[]{:S(2)}, u32[]{:S(2)}) %all-to-all-start.1) | async-done | bytes 9437216 | tf_op jit(solution)/shard_map/all_to_all | solution.py:59
  481.0 10.1 copy.8
  491.1 12.3 %fusion = f32[1536,1536]{1,0:T(8,128)} fusion(f32[1536,1536]{0,1:T(8,128)} %copy.8, f32[16,96,1536]{2,1,0:T(8,128)} %all-to-all-done.1), kind=kLoop, calls=%fused_computation.4 | loop fusion | flops 4718592 | bytes 28311552 | tf_op jit(solution)/shard_map/jit(cholesky)/div | solution.py:62
  504.2 11.7 %cholesky.341 = f32[128,128]{1,0:T(8,128)S(1)} custom-call(f32[128,128]{1,0:T(8,128)S(1)} %cholesky.892), custom_call_target="Cholesky" | custom-call | tf_op jit(solution)/shard_map/jit(cholesky)/cholesky | solution.py:62
  520.8 9.8 custom-call.98
  535.3 11.9 %cholesky.362 = f32[128,128]{1,0:T(8,128)S(1)} custom-call(f32[128,128]{1,0:T(8,128)S(1)} %cholesky.896), custom_call_target="Cholesky" | custom-call | tf_op jit(solution)/shard_map/jit(cholesky)/cholesky | solution.py:62
  547.8 9.8 custom-call.99
  562.0 11.7 %cholesky.385 = f32[128,128]{1,0:T(8,128)S(1)} custom-call(f32[128,128]{1,0:T(8,128)S(1)} %cholesky.901), custom_call_target="Cholesky" | custom-call | tf_op jit(solution)/shard_map/jit(cholesky)/cholesky | solution.py:62
  574.4 10.0 custom-call.100
  589.2 11.7 %cholesky.715 = f32[128,128]{1,0:T(8,128)S(1)} custom-call(f32[128,128]{1,0:T(8,128)S(1)} %cholesky.906), custom_call_target="Cholesky" | custom-call | tf_op jit(solution)/shard_map/jit(cholesky)/cholesky | solution.py:62
  601.6 9.8 custom-call.101
  616.4 12.1 %cholesky.734 = f32[128,128]{1,0:T(8,128)S(1)} custom-call(f32[128,128]{1,0:T(8,128)S(1)} %cholesky.911), custom_call_target="Cholesky" | custom-call | tf_op jit(solution)/shard_map/jit(cholesky)/cholesky | solution.py:62
  629.2 9.8 custom-call.102
  644.1 11.7 %cholesky.754 = f32[128,128]{1,0:T(8,128)S(1)} custom-call(f32[128,128]{1,0:T(8,128)S(1)} %cholesky.916), custom_call_target="Cholesky" | custom-call | tf_op jit(solution)/shard_map/jit(cholesky)/cholesky | solution.py:62
  656.5 10.0 custom-call.103
  671.6 11.7 %cholesky.774 = f32[128,128]{1,0:T(8,128)S(1)} custom-call(f32[128,128]{1,0:T(8,128)S(1)} %cholesky.921), custom_call_target="Cholesky" | custom-call | tf_op jit(solution)/shard_map/jit(cholesky)/cholesky | solution.py:62
  684.0 9.8 custom-call.104
  699.1 11.7 %cholesky.794 = f32[128,128]{1,0:T(8,128)S(1)} custom-call(f32[128,128]{1,0:T(8,128)S(1)} %cholesky.926), custom_call_target="Cholesky" | custom-call | tf_op jit(solution)/shard_map/jit(cholesky)/cholesky | solution.py:62
  711.4 9.8 custom-call.105
  725.9 12.2 %cholesky.814 = f32[128,128]{1,0:T(8,128)S(1)} custom-call(f32[128,128]{1,0:T(8,128)S(1)} %cholesky.931), custom_call_target="Cholesky" | custom-call | tf_op jit(solution)/shard_map/jit(cholesky)/cholesky | solution.py:62
  738.7 9.8 custom-call.106
  752.9 11.7 %cholesky.834 = f32[128,128]{1,0:T(8,128)S(1)} custom-call(f32[128,128]{1,0:T(8,128)S(1)} %cholesky.936), custom_call_target="Cholesky" | custom-call | tf_op jit(solution)/shard_map/jit(cholesky)/cholesky | solution.py:62
  765.2 9.8 custom-call.107
  778.7 11.9 %cholesky.854 = f32[128,128]{1,0:T(8,128)S(1)} custom-call(f32[128,128]{1,0:T(8,128)S(1)} %cholesky.941), custom_call_target="Cholesky" | custom-call | tf_op jit(solution)/shard_map/jit(cholesky)/cholesky | solution.py:62
  791.2 9.8 custom-call.108
  804.2 11.7 %cholesky.872 = f32[128,128]{1,0:T(8,128)S(1)} custom-call(f32[128,128]{1,0:T(8,128)S(1)} %convolution_subtract_fusion.25), custom_call_target="Cholesky" | custom-call | tf_op jit(solution)/shard_map/jit(cholesky)/cholesky | solution.py:62
  840.2 35.2 %while.1 = (s32[]{:T(128)}, f32[1536,1536]{1,0:T(8,128)}, s32[12,2]{0,1:T(2,128)S(1)}, f32[12,128,128]{2,1,0:T(8,128)S(1)}, s32[]{:T(128)}) while((s32[]{:T(128)}, f32[1536,1536]{1,0:T(8,128)}, s32[12,2]{0,1:T(2,128)S(1)}, f32[12,128,128]{2,1,0:T(8,128)S(1)}, s32[]{:T(128)}) %tuple.106), condition=%wide.while_cond, body=%wide.while_body.sunk | while | flops 2 | bytes 131189 | solution.py:64
  875.4 118.3 %custom-call.109 = f32[12,128,128]{1,2,0:T(8,128)S(1)} custom-call(f32[12,128,128]{2,1,0:T(8,128)S(1)} %get-tuple-element.12), custom_call_target="InvertDiagBlocksLowerTriangular" | custom-call | tf_op jit(solution)/shard_map/jit(_solve_triangular)/triangular_solve | solution.py:64
  (222 shorter events, 172.3 us)
Async XLA Ops:
  6.5 90.4 %reduce-scatter.2.cloned.1.call-start = ((), (), s32[]{:S(2)}) async-start(), calls=%async_computation.3 | async-start | bytes 6127616 | tf_op jit(solution)/shard_map/reduce_scatter | solution.py:40
  17.2 240.3 %all-reduce.3.cloned.1.call-start = ((), (), s32[]{:S(2)}) async-start(), calls=%async_computation.4 | async-start | bytes 4325376 | tf_op jit(solution)/shard_map/psum | solution.py:56
  263.4 9.0 copy-start.1
  263.5 217.6 %all-to-all-start.1 = ((f32[16,96,1536]{2,1,0:T(8,128)}), f32[16,96,1536]{2,1,0:T(8,128)}, u32[]{:S(2)}, u32[]{:S(2)}) async-start(f32[16,96,1536]{2,1,0:T(8,128)} %stack.2), calls=%async_computation.2 | async-start | bytes 18874368 | tf_op jit(solution)/shard_map/all_to_all | solution.py:59
  995.3 9.7 copy-start
Sparse Core Ops, SparseCore 0:
  17.4 79.5 reduce-scatter.1
  127.2 130.2 all-reduce.2
